TPU v7x, 32 devices: a whole 2x2x4 slice. The times are simulated.
32 devices in a mesh: wide: 8 (over y, x, core), narrow: 4 (over z).
Axes of the slice: x: 2, y: 2, z: 4, core: 2. Of those that a mesh axis runs over, the one named last changes fastest.
Arguments:
- hidden: bfloat16 [512, 4096], P('wide', 'narrow'), may hold values from -90 to 90
- head_weights: bfloat16 [4096, 303104], P(None, ('wide', 'narrow')), may hold values from -0.09375 to 0.09375
- token_ids: int32 [256], replicated, may hold values from 0 to 151551
- kl_weight: float32 [256], replicated, may hold values from 4 to 32
- advantage: float32 [256], replicated, may hold values from -12 to 12
Outputs:
- hidden_grad: float32 [4096, 512], P('narrow', 'wide')
- mixture_lse: float32 [256], replicated
- divergence: float32 [256], replicated
All inputs are finite; a program needn't handle non-finite values.
Results may differ from a plain program's by a relative error of at most 0.012.
Values may be sent and summed in bfloat16 or wider, within the bound.
A program may use at most 192 MiB of HBM per device.

v0:
```python
import jax
import jax.numpy as jnp
from jax import lax
from jax.sharding import PartitionSpec as P

BETA = 0.2
LANES = 128
CHUNKS = 4


def partner(block, axis, bit):
    count = lax.axis_size(axis)
    route = []
    for low in range(count):
        high = low | 1 << bit
        if high != low and high < count:
            route += [(low, high), (high, low)]
    return lax.ppermute(block, axis, route)


def chunk_edges(width):
    blocks = -(-width // LANES)
    parts = min(CHUNKS, blocks)
    return [min(width, (blocks * i + parts - 1) // parts * LANES) for i in range(parts + 1)]


def body(hidden, head_weights, token_ids, kl_weight, advantage):
    wide_count = lax.axis_size("wide")
    narrow_count = lax.axis_size("narrow")
    half_count = wide_count // 2
    half_bits = half_count.bit_length() - 1
    wide_index = lax.axis_index("wide")
    narrow_index = lax.axis_index("narrow")
    is_reference = wide_index >= half_count
    block_width = head_weights.shape[1]
    col_start = (wide_index % half_count * narrow_count + narrow_index) * block_width
    edges = chunk_edges(block_width)
    spans = list(zip(edges[:-1], edges[1:]))

    gathered = lax.all_gather(hidden, "narrow", axis=1, tiled=True)
    for bit_number in reversed(range(half_bits)):
        partner_rows = partner(gathered, "wide", bit_number)
        upper_bit = wide_index // (1 << bit_number) % 2 == 1
        gathered = jnp.where(
            upper_bit,
            jnp.concatenate([partner_rows, gathered], 0),
            jnp.concatenate([gathered, partner_rows], 0),
        )
    row_total = gathered.shape[0]
    mid = row_total // 2

    def reverse_blocks(rows):
        split = rows.reshape((2,) * half_bits + (-1,))
        return split.transpose(tuple(reversed(range(half_bits))) + (half_bits,)).reshape(-1)

    def own_rows(rows):
        return jnp.where(is_reference, rows[mid:], rows[:mid])

    ids = own_rows(reverse_blocks(token_ids))[:, None]
    kl = own_rows(reverse_blocks(kl_weight))[:, None]
    adv = own_rows(reverse_blocks(advantage))[:, None]

    kept, received = [], []
    for low, high in spans:
        logits = jnp.dot(gathered, head_weights[:, low:high], preferred_element_type=jnp.float32)
        sent = jnp.where(is_reference, logits[:mid], logits[mid:])
        received.append(partner(sent, "wide", half_bits))
        kept.append(own_rows(logits))
    pairs, stats = [], []
    for own, other in zip(kept, received):
        policy = jnp.where(is_reference, other, own)
        ref = jnp.where(is_reference, own, other)
        mixed = (1.0 - BETA) * policy + BETA * ref
        p_top, m_top = jnp.max(policy, 1), jnp.max(mixed, 1)
        p_exp = jnp.exp(policy - p_top[:, None])
        m_exp = jnp.exp(mixed - m_top[:, None])
        stats.append(
            jnp.stack(
                [
                    p_top,
                    m_top,
                    jnp.sum(p_exp, 1),
                    jnp.sum(m_exp, 1),
                    jnp.sum(p_exp * (policy - mixed), 1),
                ]
            )
        )
        pairs.append((policy, mixed))

    def combine(parts):
        p_tops, m_tops, p_sums, m_sums, crosses = (parts[:, i] for i in range(5))
        p_top, m_top = jnp.max(p_tops, 0), jnp.max(m_tops, 0)
        p_scale, m_scale = jnp.exp(p_tops - p_top), jnp.exp(m_tops - m_top)
        return jnp.stack(
            [
                p_top,
                m_top,
                jnp.sum(p_sums * p_scale, 0),
                jnp.sum(m_sums * m_scale, 0),
                jnp.sum(crosses * p_scale, 0),
            ]
        )

    everyone = lax.all_gather(combine(jnp.stack(stats)), ("wide", "narrow"), axis=0, tiled=False)
    device_half = half_count * narrow_count
    total = jnp.concatenate(
        [combine(everyone[:device_half]), combine(everyone[device_half:])], 1
    )
    policy_lse_all = total[0] + jnp.log(total[2])
    mixture_lse_all = total[1] + jnp.log(total[3])
    divergence_all = total[4] / total[2] - policy_lse_all + mixture_lse_all
    policy_lse = own_rows(policy_lse_all)[:, None]
    mixture_lse = own_rows(mixture_lse_all)[:, None]
    divergence = own_rows(divergence_all)[:, None]

    own_grads, other_grads = [], []
    for (low, high), (policy, mixed) in zip(spans, pairs):
        policy_prob = jnp.exp(policy - policy_lse)
        mixture_prob = jnp.exp(mixed - mixture_lse)
        log_gap = policy - policy_lse - mixed + mixture_lse
        chosen = (
            ids == col_start + low + jnp.arange(high - low, dtype=jnp.int32)[None, :]
        ).astype(jnp.float32)
        prob_shift = mixture_prob - policy_prob
        policy_grad = (
            kl * (policy_prob * (log_gap - divergence) + (1.0 - BETA) * prob_shift)
            - adv * (chosen - policy_prob)
        ).astype(jnp.bfloat16)
        ref_grad = (BETA * kl * prob_shift).astype(jnp.bfloat16)
        own_grads.append(jnp.where(is_reference, ref_grad, policy_grad))
        other_grads.append(
            partner(jnp.where(is_reference, policy_grad, ref_grad), "wide", half_bits)
        )
    contract = (((1,), (1,)), ((), ()))
    summed = None
    for (low, high), own, other in zip(spans, own_grads, other_grads):
        grad = jnp.where(
            is_reference, jnp.concatenate([other, own], 0), jnp.concatenate([own, other], 0)
        )
        term = lax.dot_general(
            head_weights[:, low:high], grad, contract, preferred_element_type=jnp.float32
        )
        summed = term if summed is None else summed + term
    for bit_number in range(half_bits):
        half_size = summed.shape[1] // 2
        upper_bit = wide_index // (1 << bit_number) % 2 == 1
        kept_half = jnp.where(upper_bit, summed[:, half_size:], summed[:, :half_size])
        sent_half = jnp.where(upper_bit, summed[:, :half_size], summed[:, half_size:])
        summed = kept_half + partner(sent_half.astype(jnp.bfloat16), "wide", bit_number).astype(
            jnp.float32
        )
    summed = lax.psum_scatter(
        summed.astype(jnp.bfloat16), "narrow", scatter_dimension=0, tiled=True
    ).astype(jnp.float32)
    return (summed, reverse_blocks(mixture_lse_all), reverse_blocks(divergence_all))


def solution(mesh):
    return jax.shard_map(
        body,
        mesh=mesh,
        in_specs=(P("wide", "narrow"), P(None, ("wide", "narrow")), P(), P(), P()),
        out_specs=(P("narrow", "wide"), P(), P()),
        check_vma=False,
    )
```

profile of v0, /device:TPU:1, one launch (start us, length us, event | category | flops | bytes accessed | tf_op | source)
XLA Modules:
  0.0 365.7 jit_solution(2627147423260389254)
XLA Ops:
  7.2 15.5 %all_gather.9 = bf16[64,4096]{1,0:T(8,128)(2,1)S(1)} all-gather(bf16[64,1024]{1,0:T(8,128)(2,1)} %param.5), channel_id=1, replica_groups=mesh['wide'=8,'narrow'=4] {'narrow'}, dimensions={1}, use_global_device_ids=true | all-gather | bytes 655360 | tf_op jit(solution)/shard_map/all_gather | solution.py:40
  22.8 1.3 collective-permute-start
  24.0 10.2 %collective-permute-done = bf16[64,4096]{1,0:T(8,128)(2,1)S(1)} collective-permute-done((bf16[64,4096]{1,0:T(8,128)(2,1)S(1)}, bf16[64,4096]{1,0:T(8,128)(2,1)S(1)}, u32[]{:S(2)}, u32[]{:S(2)}) %collective-permute-start) | collective-permute-done | bytes 524320 | tf_op jit(solution)/shard_map/ppermute | solution.py:18
  34.3 0.2 maximum_select_fusion.9
  34.5 3.0 collective-permute-start.1
  37.6 0.6 select_n.303
  38.4 0.6 select_n.301
  39.0 0.6 iota_add_fusion.2
  39.7 0.6 iota_add_fusion.1
  40.3 0.6 iota_add_fusion
  40.8 0.5 broadcast_multiply_fusion
  41.3 12.9 %fusion.14 = f32[256,2304]{1,0:T(8,128)S(1)} fusion(bf16[4096,9472]{1,0:T(8,128)(2,1)} %param.6, bf16[128,4096]{1,0:T(8,128)(2,1)S(1)} %maximum_select_fusion.9, bf16[128,4096]{1,0:T(8,128)(2,1)} %collective-permute-done.1, pred[]{:T(512)S(6)} %eq.31), kind=kOutput, calls=%fused_computation.14 | convolution fusion | flops 4841275392 | bytes 23330816 | tf_op jit(solution)/shard_map/dot_general | solution.py:65
  54.4 1.3 copy-done.9
  55.7 1.2 collective-permute-start.3
  56.9 12.8 %fusion.10 = f32[256,2304]{1,0:T(8,128)S(1)} fusion(bf16[4096,9472]{1,0:T(8,128)(2,1)} %param.6, bf16[128,4096]{1,0:T(8,128)(2,1)S(1)} %maximum_select_fusion.9, bf16[128,4096]{1,0:T(8,128)(2,1)} %collective-permute-done.1, pred[]{:T(512)S(6)} %eq.31), kind=kOutput, calls=%fused_computation.10 | convolution fusion | flops 4841275392 | bytes 23330816 | tf_op jit(solution)/shard_map/dot_general | solution.py:65
  69.8 1.3 slice_select_fusion.5
  71.0 0.5 copy-done.8
  71.5 0.2 collective-permute-start.5
  71.8 13.7 %fusion.2 = f32[256,2432]{1,0:T(8,128)S(1)} fusion(bf16[4096,9472]{1,0:T(8,128)(2,1)} %param.6, bf16[128,4096]{1,0:T(8,128)(2,1)S(1)} %maximum_select_fusion.9, bf16[128,4096]{1,0:T(8,128)(2,1)} %collective-permute-done.1, pred[]{:T(512)S(6)} %eq.31), kind=kOutput, calls=%fused_computation.2 | convolution fusion | flops 5109710848 | bytes 24510464 | tf_op jit(solution)/shard_map/dot_general | solution.py:65
  85.4 1.4 slice_select_fusion.1
  86.8 0.6 copy-done.7
  87.4 1.2 collective-permute-start.4
  88.6 13.8 %fusion.6 = f32[256,2432]{1,0:T(8,128)S(1)} fusion(bf16[4096,9472]{1,0:T(8,128)(2,1)} %param.6, bf16[128,4096]{1,0:T(8,128)(2,1)S(1)} %maximum_select_fusion.9, bf16[128,4096]{1,0:T(8,128)(2,1)} %collective-permute-done.1, pred[]{:T(512)S(6)} %eq.31), kind=kOutput, calls=%fused_computation.6 | convolution fusion | flops 5109710848 | bytes 24510464 | tf_op jit(solution)/shard_map/dot_general | solution.py:65
  102.5 1.2 slice_select_fusion.3
  103.6 0.7 copy-done.6
  104.4 0.2 collective-permute-start.2
  104.6 0.9 copy-done.10
  105.5 0.9 fusion.75
  106.4 0.9 reduce_max.128
  107.3 1.3 collective-permute-done.5
  108.6 3.3 fusion.77
  111.9 0.8 reduce_max.132
  112.6 1.8 multiply_reduce_fusion.3
  114.5 0.7 stack.153
  115.2 1.9 multiply_reduce_fusion.2
  117.1 18.2 %collective-permute-done.4 = f32[128,2432]{1,0:T(8,128)} collective-permute-done((f32[128,2432]{1,0:T(8,128)}, f32[128,2432]{1,0:T(8,128)}, u32[]{:S(2)}, u32[]{:S(2)}) %collective-permute-start.4) | collective-permute-done | bytes 1245216 | tf_op jit(solution)/shard_map/ppermute | solution.py:18
  135.3 3.4 fusion.76
  138.8 23.1 %collective-permute-done.2 = f32[128,2432]{1,0:T(8,128)} collective-permute-done((f32[128,2432]{1,0:T(8,128)}, f32[128,2432]{1,0:T(8,128)}, u32[]{:S(2)}, u32[]{:S(2)}) %collective-permute-start.2) | collective-permute-done | bytes 1245216 | tf_op jit(solution)/shard_map/ppermute | solution.py:18
  161.9 3.4 fusion.74
  165.4 2.0 multiply_reduce_fusion
  167.5 0.6 multiply_reduce_fusion.1
  168.3 63.2 %all-gather.1 = f32[32,5,128]{2,1,0:T(8,128)S(1)} all-gather(f32[1,5,128]{2,1,0:T(8,128)S(1)} %bitcast.114), channel_id=2, replica_groups=mesh['wide'=8,'narrow'=4] {'wide','narrow'}, dimensions={0}, use_global_device_ids=true | all-gather | bytes 84480 | tf_op jit(solution)/shard_map/all_gather | solution.py:104
  231.8 0.5 broadcast.119
  232.3 0.6 fusion.72
  233.1 3.8 %broadcast_select_fusion.9 = (bf16[128,2304]{1,0:T(8,128)(2,1)S(1)}, bf16[128,2304]{1,0:T(8,128)(2,1)S(1)}, bf16[128,2304]{1,0:T(8,128)(2,1)S(1)}, bf16[128,2304...) fusion(pred[]{:T(512)S(6)} %ge.3, s32[2304]{0:T(1024)S(1)} %copy-done.12, ...), kind=kLoop, calls=%fused_computation.103 | loop fusion | flops 11206656 | bytes 8279553 | tf_op jit(solution)/shard_map/jit(_where)/select_n | solution.py:132
  236.9 1.5 collective-permute-start.9
  238.4 2.1 broadcast_select_fusion.3
  240.6 1.4 collective-permute-start.8
  242.3 17.1 %collective-permute-done.9 = bf16[128,2304]{1,0:T(8,128)(2,1)S(1)} collective-permute-done((bf16[128,2304]{1,0:T(8,128)(2,1)S(1)}, bf16[128,2304]{1,0:T(8,128)(2,1)S(1)}, u32[]{:S(2)}, u32[]{:S(2)}) %collective-permute-start.9) | collective-permute-done | bytes 589856 | tf_op jit(solution)/shard_map/ppermute | solution.py:18
  259.4 10.4 %fusion.8 = f32[256,4096]{1,0:T(8,128)} fusion(bf16[4096,9472]{1,0:T(8,128)(2,1)} %param.6, bf16[128,2304]{1,0:T(8,128)(2,1)S(1)} %get-tuple-element.76, bf16[128,2304]{1,0:T(8,128)(2,1)S(1)} %collective-permute-done.9, pred[]{:T(512)S(6)} %ge.3), kind=kOutput, calls=%fused_computation.8 | convolution fusion | flops 4837146624 | bytes 24248320 | tf_op jit(solution)/shard_map/dot_general | solution.py:140
  269.8 10.6 %fusion.12 = f32[256,4096]{1,0:T(8,128)} fusion(bf16[4096,9472]{1,0:T(8,128)(2,1)} %param.6, bf16[128,2304]{1,0:T(8,128)(2,1)S(1)} %get-tuple-element.77, bf16[128,2304]{1,0:T(8,128)(2,1)S(1)} %collective-permute-done.7, pred[]{:T(512)S(6)} %ge.3), kind=kOutput, calls=%fused_computation.12 | convolution fusion | flops 4837146624 | bytes 24248320 | tf_op jit(solution)/shard_map/dot_general | solution.py:140
  280.3 5.7 %collective-permute-done.8 = bf16[128,2432]{1,0:T(8,128)(2,1)S(1)} collective-permute-done((bf16[128,2432]{1,0:T(8,128)(2,1)S(1)}, bf16[128,2432]{1,0:T(8,128)(2,1)S(1)}, u32[]{:S(2)}, u32[]{:S(2)}) %collective-permute-start.8) | collective-permute-done | bytes 622624 | tf_op jit(solution)/shard_map/ppermute | solution.py:18
  286.1 11.2 %fusion = f32[256,4096]{1,0:T(8,128)} fusion(bf16[4096,9472]{1,0:T(8,128)(2,1)} %param.6, bf16[128,2432]{1,0:T(8,128)(2,1)S(1)} %get-tuple-element.74, bf16[128,2432]{1,0:T(8,128)(2,1)S(1)} %collective-permute-done.8, pred[]{:T(512)S(6)} %ge.3), kind=kOutput, calls=%fused_computation | convolution fusion | flops 5105876992 | bytes 25362432 | tf_op jit(solution)/shard_map/dot_general | solution.py:140
  297.3 15.3 %fusion.25 = f32[4096,256]{0,1:T(8,128)} fusion(f32[256,4096]{1,0:T(8,128)} %fusion.8, f32[256,4096]{1,0:T(8,128)} %fusion, f32[256,4096]{1,0:T(8,128)} %fusion.12, bf16[4096,9472]{1,0:T(8,128)(2,1)} %param.6, bf16[128,2432]{1,0:T(8,128)(2,1)S(1)} %get-tuple-element.75, bf16[128,2432]{1,0:T(8,128)(2,1)S(1)} %collective-permute-done.6, pred[]{:T(512)S(6)} %ge.3), kind=kOutput, calls=%fused_computation.19 | convolution fusion | flops 5109022720 | bytes 37945344 | tf_op jit(solution)/shard_map/dot_general | solution.py:140
  312.6 2.4 select_convert_fusion
  315.1 6.0 %collective-permute-start.10 = (bf16[4096,128]{0,1:T(8,128)(2,1)S(1)}, bf16[4096,128]{0,1:T(8,128)(2,1)S(1)}, u32[]{:S(2)}, u32[]{:S(2)}) collective-permute-start(bf16[4096,128]{0,1:T(8,128)(2,1)S(1)} %select_convert_fusion), channel_id=1, source_target_pairs={{0,4},{4,0},{8,12},{12,8},{16,20},{20,16},{24,28},{28,24},{1,5},{5... | collective-permute-start | bytes 3145736 | tf_op jit(solution)/shard_map/ppermute | solution.py:18
  321.0 2.3 collective-permute-done.10
  323.3 2.6 convert_add_fusion
  326.1 13.1 %collective-permute-done.11 = bf16[4096,64]{0,1:T(8,128)(2,1)S(1)} collective-permute-done((bf16[4096,64]{0,1:T(8,128)(2,1)S(1)}, bf16[4096,64]{0,1:T(8,128)(2,1)S(1)}, u32[]{:S(2)}, u32[]{:S(2)}) %collective-permute-start.11) | collective-permute-done | bytes 524320 | tf_op jit(solution)/shard_map/ppermute | solution.py:18
  339.2 1.0 add_convert_fusion
  340.4 0.6 reshape.144
  341.0 0.6 reshape.143
  341.7 15.6 %reduce-scatter.2.cloned.1.call-done = bf16[1024,64]{0,1:T(8,128)(2,1)} async-done(((bf16[4096,64]{0,1:T(8,128)(2,1)}), bf16[1024,64]{0,1:T(8,128)(2,1)}) %reduce-scatter.2.cloned.1.call-update) | async-done | bytes 131088 | tf_op jit(solution)/shard_map/reduce_scatter | solution.py:152
  357.2 1.6 convert_element_type.71
  (92 shorter events, 2.3 us)
Async XLA Ops:
  7.2 350.1 %reduce-scatter.2.cloned.1.call-start = ((), (), s32[]{:S(2)}) async-start(), calls=%async_computation.1 | async-start | bytes 655360 | tf_op jit(solution)/shard_map/reduce_scatter | solution.py:152
  22.7 14.7 %copy-start.20 = (s32[256]{0:T(256)S(1)}, s32[256]{0:T(256)}, u32[]{:S(2)}) copy-start(s32[256]{0:T(256)} %param.7) | copy-start | bytes 3076
  22.8 15.4 %copy-start.21 = (f32[256]{0:T(256)S(1)}, f32[256]{0:T(256)}, u32[]{:S(2)}) copy-start(f32[256]{0:T(256)} %param.8) | copy-start | bytes 3076
  22.8 15.6 %copy-start.22 = (f32[256]{0:T(256)S(1)}, f32[256]{0:T(256)}, u32[]{:S(2)}) copy-start(f32[256]{0:T(256)} %param.9) | copy-start | bytes 3076
  22.8 11.5 %collective-permute-start = (bf16[64,4096]{1,0:T(8,128)(2,1)S(1)}, bf16[64,4096]{1,0:T(8,128)(2,1)S(1)}, u32[]{:S(2)}, u32[]{:S(2)}) collective-permute-start(bf16[64,4096]{1,0:T(8,128)(2,1)S(1)} %all_gather.9), channel_id=1, source_target_pairs={{0,8},{8,0},{4,12},{12,4},{16,24},{24,16},{20,28},{28,20},{1,9},{9... | collective-permute-start | bytes 1572872 | tf_op jit(solution)/shard_map/ppermute | solution.py:18
  34.5 6.8 %collective-permute-start.1 = (bf16[128,4096]{1,0:T(8,128)(2,1)S(1)}, bf16[128,4096]{1,0:T(8,128)(2,1)}, u32[]{:S(2)}, u32[]{:S(2)}) collective-permute-start(bf16[128,4096]{1,0:T(8,128)(2,1)S(1)} %maximum_select_fusion.9), channel_id=1, source_target_pairs={{0,4},{4,0},{8,12},{12,8},{16,20},{20,16},{24,28},{28,24},{1,5},{5... | collective-permute-start | bytes 3145736 | tf_op jit(solution)/shard_map/ppermute | solution.py:18
  38.3 15.9 %copy-start.16 = (f32[128]{0:T(128)}, f32[128]{0:T(128)S(1)}, u32[]{:S(2)}) copy-start(f32[128]{0:T(128)S(1)} %select_n.271) | copy-start | bytes 1540
  54.2 1.5 copy-start.9
  55.7 48.9 %collective-permute-start.3 = (f32[128,2304]{1,0:T(8,128)S(1)}, f32[128,2304]{1,0:T(8,128)S(1)}, u32[]{:S(2)}, u32[]{:S(2)}) collective-permute-start(f32[128,2304]{1,0:T(8,128)S(1)} %slice_select_fusion.7), channel_id=1, source_target_pairs={{0,16},{16,0},{4,20},{20,4},{8,24},{24,8},{12,28},{28,12},{1,17},{... | collective-permute-start | bytes 3538952 | tf_op jit(solution)/shard_map/ppermute | solution.py:18
  69.8 1.8 copy-start.8
  71.5 37.0 %collective-permute-start.5 = (f32[128,2304]{1,0:T(8,128)}, f32[128,2304]{1,0:T(8,128)}, u32[]{:S(2)}, u32[]{:S(2)}) collective-permute-start(f32[128,2304]{1,0:T(8,128)} %slice_select_fusion.5), channel_id=1, source_target_pairs={{0,16},{16,0},{4,20},{20,4},{8,24},{24,8},{12,28},{28,12},{1,17},{... | collective-permute-start | bytes 3538952 | tf_op jit(solution)/shard_map/ppermute | solution.py:18
  85.4 2.0 copy-start.7
  87.4 47.8 %collective-permute-start.4 = (f32[128,2432]{1,0:T(8,128)}, f32[128,2432]{1,0:T(8,128)}, u32[]{:S(2)}, u32[]{:S(2)}) collective-permute-start(f32[128,2432]{1,0:T(8,128)} %slice_select_fusion.1), channel_id=1, source_target_pairs={{0,16},{16,0},{4,20},{20,4},{8,24},{24,8},{12,28},{28,12},{1,17},{... | collective-permute-start | bytes 3735560 | tf_op jit(solution)/shard_map/ppermute | solution.py:18
  102.5 1.9 copy-start.6
  102.5 3.0 copy-start.10
  104.4 57.6 %collective-permute-start.2 = (f32[128,2432]{1,0:T(8,128)}, f32[128,2432]{1,0:T(8,128)}, u32[]{:S(2)}, u32[]{:S(2)}) collective-permute-start(f32[128,2432]{1,0:T(8,128)} %slice_select_fusion.3), channel_id=1, source_target_pairs={{0,16},{16,0},{4,20},{20,4},{8,24},{24,8},{12,28},{28,12},{1,17},{... | collective-permute-start | bytes 3735560 | tf_op jit(solution)/shard_map/ppermute | solution.py:18
  106.4 6.2 %copy-start = (f32[128,2304]{1,0:T(8,128)}, f32[128,2304]{1,0:T(8,128)S(1)}, u32[]{:S(2)}) copy-start(f32[128,2304]{1,0:T(8,128)S(1)} %get-tuple-element.42) | copy-start | bytes 3538948
  106.4 6.2 %copy-start.5 = (f32[128,2304]{1,0:T(8,128)}, f32[128,2304]{1,0:T(8,128)S(1)}, u32[]{:S(2)}) copy-start(f32[128,2304]{1,0:T(8,128)S(1)} %get-tuple-element.41) | copy-start | bytes 3538948
  111.9 3.3 copy-start.1
  114.5 2.6 copy-start.14
  165.4 2.0 copy-start.3
  167.5 65.5 %copy-start.12 = (s32[2304]{0:T(1024)S(1)}, s32[2304]{0:T(1024)}, u32[]{:S(2)}) copy-start(s32[2304]{0:T(1024)} %iota_add_fusion.2) | copy-start | bytes 27652
  167.5 65.5 %copy-start.13 = (s32[2304]{0:T(1024)S(1)}, s32[2304]{0:T(1024)}, u32[]{:S(2)}) copy-start(s32[2304]{0:T(1024)} %iota_add_fusion) | copy-start | bytes 27652
  167.5 65.5 %copy-start.15 = (s32[128]{0:T(128)S(1)}, s32[128]{0:T(128)}, u32[]{:S(2)}) copy-start(s32[128]{0:T(128)} %select_n.303) | copy-start | bytes 1540
  167.5 65.5 %copy-start.17 = (f32[128]{0:T(128)S(1)}, f32[128]{0:T(128)}, u32[]{:S(2)}) copy-start(f32[128]{0:T(128)} %copy-done.16) | copy-start | bytes 1540
  167.5 65.5 %copy-start.18 = (f32[128]{0:T(128)S(1)}, f32[128]{0:T(128)}, u32[]{:S(2)}) copy-start(f32[128]{0:T(128)} %select_n.301) | copy-start | bytes 1540
  167.5 65.5 %copy-start.19 = (f32[128]{0:T(128)S(1)}, f32[128]{0:T(128)}, u32[]{:S(2)}) copy-start(f32[128]{0:T(128)} %broadcast_multiply_fusion) | copy-start | bytes 1540
  233.0 5.3 %copy-start.2 = (f32[128,2432]{1,0:T(8,128)S(1)}, f32[128,2432]{1,0:T(8,128)}, u32[]{:S(2)}) copy-start(f32[128,2432]{1,0:T(8,128)} %get-tuple-element.44) | copy-start | bytes 3735556
  233.0 5.3 %copy-start.4 = (f32[128,2432]{1,0:T(8,128)S(1)}, f32[128,2432]{1,0:T(8,128)}, u32[]{:S(2)}) copy-start(f32[128,2432]{1,0:T(8,128)} %get-tuple-element.38) | copy-start | bytes 3735556
  233.1 5.3 %copy-start.11 = (s32[2432]{0:T(1024)S(1)}, s32[2432]{0:T(1024)}, u32[]{:S(2)}) copy-start(s32[2432]{0:T(1024)} %iota_add_fusion.1) | copy-start | bytes 29188
  236.8 32.9 %collective-permute-start.7 = (bf16[128,2304]{1,0:T(8,128)(2,1)S(1)}, bf16[128,2304]{1,0:T(8,128)(2,1)S(1)}, u32[]{:S(2)}, u32[]{:S(2)}) collective-permute-start(bf16[128,2304]{1,0:T(8,128)(2,1)S(1)} %get-tuple-element.28), channel_id=1, source_target_pairs={{0,16},{16,0},{4,20},{20,4},{8,24},{24,8},{12,28},{28,12},{1,17},{... | collective-permute-start | bytes 1769480 | tf_op jit(solution)/shard_map/ppermute | solution.py:18
  236.9 22.5 %collective-permute-start.9 = (bf16[128,2304]{1,0:T(8,128)(2,1)S(1)}, bf16[128,2304]{1,0:T(8,128)(2,1)S(1)}, u32[]{:S(2)}, u32[]{:S(2)}) collective-permute-start(bf16[128,2304]{1,0:T(8,128)(2,1)S(1)} %get-tuple-element.69), channel_id=1, source_target_pairs={{0,16},{16,0},{4,20},{20,4},{8,24},{24,8},{12,28},{28,12},{1,17},{... | collective-permute-start | bytes 1769480 | tf_op jit(solution)/shard_map/ppermute | solution.py:18
  240.5 56.8 %collective-permute-start.6 = (bf16[128,2432]{1,0:T(8,128)(2,1)S(1)}, bf16[128,2432]{1,0:T(8,128)(2,1)S(1)}, u32[]{:S(2)}, u32[]{:S(2)}) collective-permute-start(bf16[128,2432]{1,0:T(8,128)(2,1)S(1)} %get-tuple-element.25), channel_id=1, source_target_pairs={{0,16},{16,0},{4,20},{20,4},{8,24},{24,8},{12,28},{28,12},{1,17},{... | collective-permute-start | bytes 1867784 | tf_op jit(solution)/shard_map/ppermute | solution.py:18
  240.6 45.4 %collective-permute-start.8 = (bf16[128,2432]{1,0:T(8,128)(2,1)S(1)}, bf16[128,2432]{1,0:T(8,128)(2,1)S(1)}, u32[]{:S(2)}, u32[]{:S(2)}) collective-permute-start(bf16[128,2432]{1,0:T(8,128)(2,1)S(1)} %get-tuple-element.66), channel_id=1, source_target_pairs={{0,16},{16,0},{4,20},{20,4},{8,24},{24,8},{12,28},{28,12},{1,17},{... | collective-permute-start | bytes 1867784 | tf_op jit(solution)/shard_map/ppermute | solution.py:18
  315.1 8.2 %collective-permute-start.10 = (bf16[4096,128]{0,1:T(8,128)(2,1)S(1)}, bf16[4096,128]{0,1:T(8,128)(2,1)S(1)}, u32[]{:S(2)}, u32[]{:S(2)}) collective-permute-start(bf16[4096,128]{0,1:T(8,128)(2,1)S(1)} %select_convert_fusion), channel_id=1, source_target_pairs={{0,4},{4,0},{8,12},{12,8},{16,20},{20,16},{24,28},{28,24},{1,5},{5... | collective-permute-start | bytes 3145736 | tf_op jit(solution)/shard_map/ppermute | solution.py:18
  326.0 13.2 %collective-permute-start.11 = (bf16[4096,64]{0,1:T(8,128)(2,1)S(1)}, bf16[4096,64]{0,1:T(8,128)(2,1)S(1)}, u32[]{:S(2)}, u32[]{:S(2)}) collective-permute-start(bf16[4096,64]{0,1:T(8,128)(2,1)S(1)} %select_convert_fusion.1), channel_id=1, source_target_pairs={{0,8},{8,0},{4,12},{12,4},{16,24},{24,16},{20,28},{28,20},{1,9},{9... | collective-permute-start | bytes 1572872 | tf_op jit(solution)/shard_map/ppermute | solution.py:18
Sparse Core Ops, SparseCore 0:
  340.3 16.8 reduce-scatter.1
where the time goes:
time: 368 us; the launch traced here: 366 us
  waiting for transfers between devices  107 us (29%)
  matrix products  101 us (27%)
  blocking collectives  78.7 us (21%)
  other arithmetic  40.5 us (11%)
  starting transfers between devices  16.3 us (4%)
  between operations  14.4 us (4%)
  local copies, waits for them, and re-layouts  8.47 us (2%)
    ppermute x12, waiting for transfers between devices, partner(): return lax.ppermute(block, axis, route)  91 us
    all_gather x1, blocking collectives, body(): lax.all_gather(combine(jnp.stack(stats)), ('wide', 'narrow'), axis=0, til...  63.2 us
    dot_general x4, matrix products, body(): jnp.dot(gathered, head_weights[:, low:high], preferred_element_type=jnp.f...  53.1 us
    dot_general x4, matrix products, body(): lax.dot_general(head_weights[:, low:high], grad, contract, preferred_elem...  47.5 us
    ppermute x12, starting transfers between devices, partner(): return lax.ppermute(block, axis, route)  16.3 us
    reduce_scatter x1, waiting for transfers between devices, body(): lax.psum_scatter(summed.astype(jnp.bfloat16), 'narrow', scatter_dimension...  15.6 us
    all_gather x1, blocking collectives, body(): gathered = lax.all_gather(hidden, 'narrow', axis=1, tiled=True)  15.5 us
    reduce_max x8, other arithmetic, body(): p_top, m_top = (jnp.max(policy, 1), jnp.max(mixed, 1))  12.9 us
  transfers between devices with their start and end apart: 13, of which 9 were waited for; matrix products, arithmetic and copies ran while one was open for 27% of the time, Pallas kernels for 0%

commit v1 on v0

--- a/solution.py
+++ b/solution.py
@@ -1,11 +1,23 @@
+import functools
+
 import jax
 import jax.numpy as jnp
 from jax import lax
+from jax.experimental import pallas as pl
+from jax.experimental.pallas import tpu as pltpu
 from jax.sharding import PartitionSpec as P
 
 BETA = 0.2
 LANES = 128
 CHUNKS = 4
+WIDTH = 256
+SLOTS = 6
+AHEAD = 4
+HIDDEN_MAX = 90.0
+WEIGHT_MAX = 0.09375
+MESH = pl.DeviceIdType.MESH
+F32 = jnp.float32
+BF16 = jnp.bfloat16
 
 
 def partner(block, axis, bit):
@@ -155,9 +167,564 @@
     return (summed, reverse_blocks(mixture_lse_all), reverse_blocks(divergence_all))
 
 
+def step_kernel(
+    quarter, line, hid_ref, w_ref, ids_ref, kl_ref, adv_ref, grad_ref, row_ref,
+    h_buf, w_buf, kept, send_q, recv_q, grads, send_d, top_buf, total,
+    stat_send, stat_recv, fin_send, fin_recv,
+    core_send, core_recv, x_send, x_recv, t_buf, up_send, up_recv, down_send, down_recv,
+    w_sem, gz_up, gz_down, gz_recv, gx_send, gx_recv, gc_send, gc_recv,
+    q_send_sem, q_recv_sem, d_send_sem, d_recv_sem, s_send_sem, s_recv_sem, f_sem,
+    rc_send, rc_recv, rx_send, rx_recv, ru_send, ru_recv, rd_send, rd_recv,
+):
+    wide = lax.axis_index("wide")
+    z = lax.axis_index("narrow")
+    rows, feats = hid_ref.shape
+    depth, width = w_ref.shape
+    half = kept.shape[2]
+    chunks = width // WIDTH
+    sides = quarter // 2
+    head = wide // quarter
+    slot_q = wide % quarter
+    x, core = slot_q // 2, slot_q % 2
+    base = head * quarter
+    is_ref = head == 1
+    members = quarter * line
+    me = slot_q * line + z
+
+    def at(w, n):
+        return {"wide": w, "narrow": n}
+
+    across = at((wide + quarter) % (2 * quarter), z)
+    x_side = at(base + (1 - x) * 2 + core, z)
+    core_side = at(base + x * 2 + 1 - core, z)
+    above, below = at(wide, z + 1), at(wide, z - 1)
+
+    def peer(i):
+        return at(base + i // line, i % line)
+
+    def weights(t):
+        col = pl.multiple_of(t % chunks * WIDTH, WIDTH)
+        slot = t % SLOTS
+        return pltpu.make_async_copy(w_ref.at[:, pl.ds(col, WIDTH)], w_buf.at[slot], w_sem.at[slot])
+
+    for t in range(SLOTS - 1):
+        weights(t).start()
+
+    barrier = pltpu.get_barrier_semaphore()
+    pl.semaphore_signal(barrier, inc=1, device_id=across, device_id_type=MESH)
+
+    @pl.loop(1, members)
+    def _(i):
+        pl.semaphore_signal(
+            barrier, inc=1, device_id=peer((me + i) % members), device_id_type=MESH
+        )
+
+    pl.semaphore_wait(barrier, members)
+
+    def place(cx, cc, cz):
+        pos = (cc + head - 2 * cc * head) * sides + cx
+        return h_buf.at[
+            pl.ds(pl.multiple_of(pos * rows, rows), rows),
+            pl.ds(pl.multiple_of(cz * feats, feats), feats),
+        ]
+
+    def push(cx, cc, cz, own, send, recv, to):
+        src = hid_ref if own else place(cx, cc, cz)
+        return pltpu.make_async_remote_copy(
+            src_ref=src, dst_ref=place(cx, cc, cz), send_sem=send, recv_sem=recv,
+            device_id=to, device_id_type=MESH,
+        )
+
+    def g_up(cz, own=False):
+        return push(x, core, cz, own, gz_up.at[cz], gz_recv.at[cz], above)
+
+    def g_down(cz, own=False):
+        return push(x, core, cz, own, gz_down.at[cz], gz_recv.at[cz], below)
+
+    def g_x(cz, own=False):
+        return push(x, core, cz, own, gx_send.at[cz], gx_recv.at[cz], x_side)
+
+    def g_x_in(cz):
+        return push(1 - x, core, cz, False, gx_send.at[cz], gx_recv.at[cz], x_side)
+
+    def g_c(cx, cz, own=False):
+        return push(cx, core, cz, own, gc_send.at[cx, cz], gc_recv.at[cx, cz], core_side)
+
+    def g_c_in(cx, cz):
+        return push(cx, 1 - core, cz, False, gc_send.at[cx, cz], gc_recv.at[cx, cz], core_side)
+
+    @pl.when(z < line - 1)
+    def _():
+        g_up(z, True).start()
+
+    @pl.when(z > 0)
+    def _():
+        g_down(z, True).start()
+
+    g_x(z, True).start()
+    g_c(x, z, True).start()
+    place(x, core, z)[...] = hid_ref[...]
+
+    def from_x(cz):
+        g_x_in(cz).wait_recv()
+        g_c(1 - x, cz).start()
+
+    for s in range(1, line):
+        @pl.when(z - s >= 0)
+        def _():
+            g_up(z - s).wait_recv()
+
+            @pl.when(z < line - 1)
+            def _():
+                g_up(z - s).start()
+
+            g_x(z - s).start()
+            g_c(x, z - s).start()
+
+        @pl.when(z + s < line)
+        def _():
+            g_down(z + s).wait_recv()
+
+            @pl.when(z > 0)
+            def _():
+                g_down(z + s).start()
+
+            g_x(z + s).start()
+            g_c(x, z + s).start()
+
+        if s == 1:
+            from_x(z)
+        else:
+            @pl.when(z - s + 1 >= 0)
+            def _():
+                from_x(z - s + 1)
+
+            @pl.when(z + s - 1 < line)
+            def _():
+                from_x(z + s - 1)
+
+    last = line - 1
+
+    if last > 0:
+        @pl.when(z - last >= 0)
+        def _():
+            from_x(z - last)
+
+        @pl.when(z + last < line)
+        def _():
+            from_x(z + last)
+    else:
+        from_x(z)
+
+    total[...] = jnp.zeros_like(total)
+    top_buf[...] = jnp.full_like(top_buf, -1e30)
+    for cz in range(line):
+        for cx in range(sides):
+            g_c_in(cx, cz).wait_recv()
+
+    reach = 2.0 * depth * HIDDEN_MAX * WEIGHT_MAX + 2.0
+    code_scale = float(int(65500.0 / reach ** 0.25))
+
+    def q_copy(j):
+        return pltpu.make_async_remote_copy(
+            src_ref=send_q.at[j], dst_ref=recv_q.at[j], send_sem=q_send_sem.at[j],
+            recv_sem=q_recv_sem.at[j], device_id=across, device_id_type=MESH,
+        )
+
+    @pl.loop(0, chunks)
+    def _(j):
+        weights(j + SLOTS - 1).start()
+        weights(j).wait()
+        logits = jnp.dot(h_buf[...], w_buf[j % SLOTS], preferred_element_type=F32)
+        kept[j] = logits[:half].T
+        other = logits[half:].T
+        top = jnp.maximum(top_buf[...], jnp.max(other, 0, keepdims=True))
+        top_buf[...] = top
+        top_code = jnp.floor(top * 0.5) + 1.0
+        gap = jnp.sqrt(jnp.sqrt(jnp.maximum(2.0 * top_code[0:1] - other, 0.0)))
+        code = (gap * code_scale + 0.5).astype(jnp.int32) - 32768
+        send_q[j, 0:WIDTH] = code.astype(jnp.int16)
+        send_q[j, WIDTH:] = jnp.broadcast_to(
+            top_code[0:1].astype(jnp.int32), (16, half)
+        ).astype(jnp.int16)
+
+        @pl.when(j > 0)
+        def _():
+            q_copy(j - 1).start()
+
+    q_copy(chunks - 1).start()
+
+    def load_pair(j):
+        own = kept[j]
+        code = recv_q[j, 0:WIDTH].astype(jnp.int32).astype(F32) + 32768.0
+        top = recv_q[j, WIDTH:].astype(jnp.int32).astype(F32)[0:1] * 2.0
+        gap = code * (1.0 / code_scale)
+        gap = gap * gap
+        other = top - gap * gap
+        policy = jnp.where(is_ref, other, own)
+        ref = jnp.where(is_ref, own, other)
+        return policy, (1.0 - BETA) * policy + BETA * ref
+
+    def stat_step(j, carry):
+        p_top, m_top, p_sum, m_sum, cross = carry
+        q_copy(j).wait_recv()
+        policy, mixed = load_pair(j)
+        p_new = jnp.maximum(p_top, jnp.max(policy, 0, keepdims=True))
+        m_new = jnp.maximum(m_top, jnp.max(mixed, 0, keepdims=True))
+        p_exp, m_exp = jnp.exp(policy - p_new), jnp.exp(mixed - m_new)
+        p_scale, m_scale = jnp.exp(p_top - p_new), jnp.exp(m_top - m_new)
+        return (
+            p_new,
+            m_new,
+            p_sum * p_scale + jnp.sum(p_exp, 0, keepdims=True),
+            m_sum * m_scale + jnp.sum(m_exp, 0, keepdims=True),
+            cross * p_scale + jnp.sum(p_exp * (policy - mixed), 0, keepdims=True),
+        )
+
+    low = jnp.full((1, half), -1e30, F32)
+    zero = jnp.zeros((1, half), F32)
+    stats = lax.fori_loop(0, chunks, stat_step, (low, low, zero, zero, zero))
+
+    packed = jnp.concatenate(list(stats) + [zero, zero, zero], 0)
+    stat_send[...] = packed
+    stat_recv[me] = packed
+
+    def s_copy(i):
+        return pltpu.make_async_remote_copy(
+            src_ref=stat_send, dst_ref=stat_recv.at[me], send_sem=s_send_sem.at[i],
+            recv_sem=s_recv_sem.at[me], device_id=peer(i), device_id_type=MESH,
+        )
+
+    def s_copy_in(i):
+        return pltpu.make_async_remote_copy(
+            src_ref=stat_send, dst_ref=stat_recv.at[i], send_sem=s_send_sem.at[i],
+            recv_sem=s_recv_sem.at[i], device_id=peer(i), device_id_type=MESH,
+        )
+
+    @pl.loop(1, members)
+    def _(i):
+        s_copy((me + i) % members).start()
+
+    @pl.loop(1, members)
+    def _(i):
+        s_copy_in((me + i) % members).wait_recv()
+
+    p_top, m_top = low, low
+    for i in range(members):
+        p_top = jnp.maximum(p_top, stat_recv[i, 0:1])
+        m_top = jnp.maximum(m_top, stat_recv[i, 1:2])
+    p_sum, m_sum, cross = zero, zero, zero
+    for i in range(members):
+        p_scale = jnp.exp(stat_recv[i, 0:1] - p_top)
+        m_scale = jnp.exp(stat_recv[i, 1:2] - m_top)
+        p_sum += stat_recv[i, 2:3] * p_scale
+        m_sum += stat_recv[i, 3:4] * m_scale
+        cross += stat_recv[i, 4:5] * p_scale
+    policy_lse = p_top + jnp.log(p_sum)
+    mixture_lse = m_top + jnp.log(m_sum)
+    divergence = cross / p_sum - policy_lse + mixture_lse
+    finals = jnp.concatenate([mixture_lse, divergence] + [zero] * 6, 0)
+    fin_send[...] = finals
+
+    kl = kl_ref[pl.ds(head, 1), :]
+    adv = adv_ref[pl.ds(head, 1), :]
+    ids = ids_ref[pl.ds(head, 1), :] - me * width
+    col = lax.broadcasted_iota(jnp.int32, (WIDTH, half), 0)
+
+    def d_copy(j):
+        return pltpu.make_async_remote_copy(
+            src_ref=send_d.at[j], dst_ref=grads.at[j, 1], send_sem=d_send_sem.at[j],
+            recv_sem=d_recv_sem.at[j], device_id=across, device_id_type=MESH,
+        )
+
+    def grad_step(j):
+        policy, mixed = load_pair(j)
+        policy_prob = jnp.exp(policy - policy_lse)
+        mixture_prob = jnp.exp(mixed - mixture_lse)
+        log_gap = policy - policy_lse - mixed + mixture_lse
+        chosen = jnp.where(col + j * WIDTH == ids, 1.0, 0.0)
+        shift = mixture_prob - policy_prob
+        policy_grad = kl * (
+            policy_prob * (log_gap - divergence) + (1.0 - BETA) * shift
+        ) - adv * (chosen - policy_prob)
+        ref_grad = BETA * kl * shift
+        grads[j, 0] = jnp.where(is_ref, ref_grad, policy_grad).astype(BF16)
+        send_d[j] = jnp.where(is_ref, policy_grad, ref_grad).astype(BF16)
+
+        @pl.when(j > 0)
+        def _():
+            d_copy(j - 1).start()
+
+        @pl.when(j == chunks - 1)
+        def _():
+            d_copy(j).start()
+
+    @pl.loop(0, min(AHEAD, chunks))
+    def _(j):
+        grad_step(j)
+
+    f_copy = pltpu.make_async_remote_copy(
+        src_ref=fin_send, dst_ref=fin_recv, send_sem=f_sem.at[0], recv_sem=f_sem.at[1],
+        device_id=across, device_id_type=MESH,
+    )
+    f_copy.start()
+
+    block = depth // 8
+
+    @pl.loop(0, chunks)
+    def _(j):
+        @pl.when(j + AHEAD < chunks)
+        def _():
+            grad_step(j + AHEAD)
+
+        @pl.when(j + SLOTS - 1 < chunks)
+        def _():
+            weights(chunks + j + SLOTS - 1).start()
+
+        weights(chunks + j).wait()
+        d_copy(j).wait_recv()
+        rhs = jnp.concatenate([grads[j, 0], grads[j, 1]], 1)
+        slot = (chunks + j) % SLOTS
+
+        @pl.loop(0, 8)
+        def _(b):
+            span = pl.ds(pl.multiple_of(b * block, block), block)
+            term = jnp.dot(w_buf[slot, span], rhs, preferred_element_type=F32)
+            total[0, span] += term[:, :half]
+            total[1, span] += term[:, half:]
+
+    mine = core + head - 2 * core * head
+    fold = feats // 2
+    lane = lax.broadcasted_iota(jnp.int32, (fold, half), 1)
+
+    def order(k):
+        falling = line - 1 - k
+        falling = falling - jnp.where(falling <= z, 1, 0)
+        rising = k + jnp.where(k >= z, 1, 0)
+        pick = jnp.where(z < line // 2, falling, rising)
+        return jnp.where(k == line - 1, z, pick)
+
+    def span_of(cz, part=None):
+        if part is None:
+            return pl.ds(pl.multiple_of(cz * feats, feats), feats)
+        return pl.ds(pl.multiple_of(cz * feats + part * fold, fold), fold)
+
+    def hand(src, dst, send, recv, to):
+        return pltpu.make_async_remote_copy(
+            src_ref=src, dst_ref=dst, send_sem=send, recv_sem=recv,
+            device_id=to, device_id_type=MESH,
+        )
+
+    def r_core(cz):
+        return hand(core_send.at[cz], core_recv.at[cz], rc_send.at[cz], rc_recv.at[cz], core_side)
+
+    def r_x(cz):
+        return hand(x_send.at[cz], x_recv.at[cz], rx_send.at[cz], rx_recv.at[cz], x_side)
+
+    def r_up(cz):
+        return hand(up_send.at[cz], up_recv.at[cz], ru_send.at[cz], ru_recv.at[cz], above)
+
+    def r_down(cz):
+        return hand(down_send.at[cz], down_recv.at[cz], rd_send.at[cz], rd_recv.at[cz], below)
+
+    @pl.loop(0, line)
+    def _(k):
+        cz = order(k)
+        core_send[cz] = total[1 - mine, span_of(cz)].astype(BF16)
+        r_core(cz).start()
+
+    @pl.loop(0, line)
+    def _(k):
+        cz = order(k)
+        r_core(cz).wait_recv()
+        upper = total[mine, span_of(cz, 0)] + core_recv[cz, 0:fold].astype(F32)
+        lower = total[mine, span_of(cz, 1)] + core_recv[cz, fold:].astype(F32)
+        left = jnp.where(lane < rows, upper, pltpu.roll(lower, rows, 1))
+        right = jnp.where(lane < rows, pltpu.roll(upper, rows, 1), lower)
+        t_buf[cz] = jnp.where(x == 0, left, right)
+        x_send[cz] = jnp.where(x == 0, right, left).astype(BF16)
+        r_x(cz).start()
+
+    def settled(cz):
+        r_x(cz).wait_recv()
+        t_buf[cz] += x_recv[cz].astype(F32)
+
+    def go_up(cz):
+        settled(cz)
+
+        @pl.when(z > 0)
+        def _():
+            r_up(cz).wait_recv()
+            t_buf[cz] += up_recv[cz].astype(F32)
+
+        up_send[cz] = t_buf[cz].astype(BF16)
+        r_up(cz).start()
+
+    def go_down(cz):
+        settled(cz)
+
+        @pl.when(z < line - 1)
+        def _():
+            r_down(cz).wait_recv()
+            t_buf[cz] += down_recv[cz].astype(F32)
+
+        down_send[cz] = t_buf[cz].astype(BF16)
+        r_down(cz).start()
+
+    @pl.loop(0, line - 1)
+    def _(i):
+        @pl.when(line - 1 - i > z)
+        def _():
+            go_up(line - 1 - i)
+
+        @pl.when(i < z)
+        def _():
+            go_down(i)
+
+    settled(z)
+
+    @pl.when(z > 0)
+    def _():
+        r_up(z).wait_recv()
+        t_buf[z] += up_recv[z].astype(F32)
+
+    @pl.when(z < line - 1)
+    def _():
+        r_down(z).wait_recv()
+        t_buf[z] += down_recv[z].astype(F32)
+
+    done = t_buf[z]
+    grad_ref[0:fold] = done[:, 0:rows]
+    grad_ref[fold:] = pltpu.roll(done, rows, 1)[:, 0:rows]
+
+    f_copy.wait_recv()
+    theirs = fin_recv[...]
+    row_ref[0] = jnp.where(is_ref, theirs, finals)
+    row_ref[1] = jnp.where(is_ref, finals, theirs)
+
+    f_copy.wait_send()
+
+    @pl.loop(0, chunks)
+    def _(j):
+        q_copy(j).wait_send()
+        d_copy(j).wait_send()
+
+    @pl.loop(1, members)
+    def _(i):
+        s_copy((me + i) % members).wait_send()
+
+    @pl.loop(0, line)
+    def _(cz):
+        r_core(cz).wait_send()
+        r_x(cz).wait_send()
+        g_x(cz).wait_send()
+        for cx in range(sides):
+            g_c(cx, cz).wait_send()
+
+        @pl.when(cz > z)
+        def _():
+            r_up(cz).wait_send()
+
+        @pl.when(cz < z)
+        def _():
+            r_down(cz).wait_send()
+
+        @pl.when(jnp.logical_and(cz <= z, z < line - 1))
+        def _():
+            g_up(cz).wait_send()
+
+        @pl.when(jnp.logical_and(cz >= z, z > 0))
+        def _():
+            g_down(cz).wait_send()
+
+
+def fused(hidden, head_weights, token_ids, kl_weight, advantage):
+    quarter, line = lax.axis_size("wide") // 2, lax.axis_size("narrow")
+    rows, feats = hidden.shape
+    depth, width = head_weights.shape
+    tokens = rows * quarter
+    half, sides = tokens // 2, quarter // 2
+    chunks, members, fold = width // WIDTH, quarter * line, feats // 2
+
+    def split(values):
+        return values.reshape(sides, 2, rows).transpose(1, 0, 2).reshape(2, half)
+
+    def join(values):
+        return values.reshape(2, sides, rows).transpose(1, 0, 2).reshape(tokens)
+
+    vmem = pl.BlockSpec(memory_space=pltpu.VMEM)
+    dma, v = pltpu.SemaphoreType.DMA, pltpu.VMEM
+    grad, per_row = pl.pallas_call(
+        functools.partial(step_kernel, quarter, line),
+        out_shape=(
+            jax.ShapeDtypeStruct((feats, rows), F32),
+            jax.ShapeDtypeStruct((2, 8, half), F32),
+        ),
+        in_specs=[vmem, pl.BlockSpec(memory_space=pl.ANY), vmem, vmem, vmem],
+        out_specs=(vmem, vmem),
+        scratch_shapes=[
+            v((tokens, depth), BF16),
+            v((SLOTS, depth, WIDTH), BF16),
+            v((chunks, WIDTH, half), F32),
+            v((chunks, WIDTH + 16, half), jnp.int16),
+            v((chunks, WIDTH + 16, half), jnp.int16),
+            v((chunks, 2, WIDTH, half), BF16),
+            v((chunks, WIDTH, half), BF16),
+            v((8, half), F32),
+            v((2, depth, half), F32),
+            v((8, half), F32),
+            v((members, 8, half), F32),
+            v((8, half), F32),
+            v((8, half), F32),
+            v((line, feats, half), BF16),
+            v((line, feats, half), BF16),
+            v((line, fold, half), BF16),
+            v((line, fold, half), BF16),
+            v((line, fold, half), F32),
+            v((line, fold, half), BF16),
+            v((line, fold, half), BF16),
+            v((line, fold, half), BF16),
+            v((line, fold, half), BF16),
+            dma((SLOTS,)),
+            dma((line,)), dma((line,)), dma((line,)), dma((line,)), dma((line,)),
+            dma((sides, line)), dma((sides, line)),
+            dma((chunks,)), dma((chunks,)), dma((chunks,)), dma((chunks,)),
+            dma((members,)), dma((members,)), dma((2,)),
+            dma((line,)), dma((line,)), dma((line,)), dma((line,)),
+            dma((line,)), dma((line,)), dma((line,)), dma((line,)),
+        ],
+        compiler_params=pltpu.CompilerParams(
+            collective_id=0, has_side_effects=True, vmem_limit_bytes=62 * 1024 * 1024
+        ),
+        name="step",
+    )(hidden, head_weights, split(token_ids), split(kl_weight), split(advantage))
+    return grad, join(per_row[:, 0]), join(per_row[:, 1])
+
+
+def fits(quarter, line, hidden, head_weights):
+    rows, feats = hidden.shape
+    depth, width = head_weights.shape
+    return (
+        quarter == 4
+        and line >= 2
+        and rows * quarter == 2 * LANES
+        and width % WIDTH == 0
+        and width // WIDTH >= SLOTS
+        and depth % (8 * LANES) == 0
+        and feats % 32 == 0
+        and feats * line == depth
+    )
+
+
+def device_step(hidden, head_weights, token_ids, kl_weight, advantage):
+    quarter, line = lax.axis_size("wide") // 2, lax.axis_size("narrow")
+    run = fused if fits(quarter, line, hidden, head_weights) else body
+    return run(hidden, head_weights, token_ids, kl_weight, advantage)
+
+
 def solution(mesh):
     return jax.shard_map(
-        body,
+        device_step,
         mesh=mesh,
         in_specs=(P("wide", "narrow"), P(None, ("wide", "narrow")), P(), P(), P()),
         out_specs=(P("narrow", "wide"), P(), P()),

time: 368 us -> 204 us (0.55)
  Pallas kernels: 0 us -> 192 us
  waiting for transfers between devices: 107 us -> 0 us
  matrix products: 101 us -> 0 us
  blocking collectives: 78.7 us -> 0 us
  other arithmetic: 40.5 us -> 0 us
  starting transfers between devices: 16.3 us -> 0 us
  between operations: 14.4 us -> 0.65 us
    pallas_call x0 -> x1, Pallas kernels: none -> 192 us  [fused(): pl.pallas_call(functools.partial(step_kernel, quarter, line), out_shape=(...]
    dot_general x8 -> x0, matrix products: 101 us -> none  [the longest x4 53.1 us: body(): jnp.dot(gathered, head_weights[:, low:high], preferred_element_type=jnp.f...]
    ppermute x12 -> x0, waiting for transfers between devices: 91 us -> none  [partner(): return lax.ppermute(block, axis, route)]
    all_gather x2 -> x0, blocking collectives: 78.7 us -> none  [the longest x1 63.2 us: body(): lax.all_gather(combine(jnp.stack(stats)), ('wide', 'narrow'), axis=0, til...]
    ppermute x12 -> x0, starting transfers between devices: 16.3 us -> none  [partner(): return lax.ppermute(block, axis, route)]
    reduce_scatter x1 -> x0, waiting for transfers between devices: 15.6 us -> none  [body(): lax.psum_scatter(summed.astype(jnp.bfloat16), 'narrow', scatter_dimension...]
    reduce_max x14 -> x0, other arithmetic: 13 us -> none  [the longest x8 12.9 us: body(): p_top, m_top = (jnp.max(policy, 1), jnp.max(mixed, 1))]
    select_n x15 -> x0, other arithmetic: 10.4 us -> none  [the longest x2 5.88 us: body(): jnp.where(is_reference, policy_grad, ref_grad)]
  transfers between devices with their start and end apart: 13 -> 0, of which waited for: 9 -> 0; matrix products, arithmetic and copies ran while one was open for 27% -> 0% of each run, Pallas kernels for 0% -> 0%
where the time goes in v1:
time: 204 us; the launch traced here: 201 us
  Pallas kernels  192 us (94%)
  local copies, waits for them, and re-layouts  8.41 us (4%)
    pallas_call x1, Pallas kernels, fused(): pl.pallas_call(functools.partial(step_kernel, quarter, line), out_shape=(...  192 us
    reshape x6, local copies, waits for them, and re-layouts, split(): return values.reshape(sides, 2, rows).transpose(1, 0, 2).reshape(2, half)  4.21 us

profile of v1, /device:TPU:1, one launch (start us, length us, event | category | flops | bytes accessed | tf_op | source)
XLA Modules:
  0.0 200.9 jit_solution(11557928311485696434)
XLA Ops:
  0.6 0.8 reshape.30
  1.4 0.6 reshape.31.ids_ref
  2.0 0.8 reshape.32
  2.8 0.6 reshape.33.kl_ref
  3.5 0.8 reshape.34
  4.2 0.6 reshape.35.adv_ref
  4.9 191.8 %step.1 = (f32[1024,64]{1,0:T(8,128)}, f32[2,8,128]{2,1,0:T(8,128)}) custom-call(bf16[64,1024]{1,0:T(8,128)(2,1)} %hid_ref.1, bf16[4096,9472]{1,0:T(8,128)(2,1)} %w_ref.1, s32[2,128]{1,0:T(2,128)} %reshape.31.ids_ref, f32[2,128]{1,0:T(2,128)} %reshape.33.kl_ref, f32[2,128]{1,0:T(2,128)} %reshape.35.adv_ref), custom_call_target="tpu_custom_call" | custom-call | tf_op jit(solution)/shard_map/step/pallas_call | solution.py:657
  196.7 0.8 slice_reduce_fusion
  197.5 0.1 reshape_squeeze.6
  197.6 0.6 reshape.36
  198.2 0.1 reshape_squeeze.7
  198.3 0.6 reshape.37
  198.9 1.9 copy.14
  (5 shorter events, 0.0 us)

commit v2 on v1

--- a/solution.py
+++ b/solution.py
@@ -11,7 +11,10 @@
 LANES = 128
 CHUNKS = 4
 WIDTH = 256
-SLOTS = 6
+HELD = 8
+RING = 4
+BOTH = 6
+PIECES = 2
 AHEAD = 4
 HIDDEN_MAX = 90.0
 WEIGHT_MAX = 0.09375
@@ -168,13 +171,13 @@
 
 
 def step_kernel(
-    quarter, line, hid_ref, w_ref, ids_ref, kl_ref, adv_ref, grad_ref, row_ref,
-    h_buf, w_buf, kept, send_q, recv_q, grads, send_d, top_buf, total,
+    quarter, line, hid_ref, w_ref, ids_ref, kl_ref, adv_ref, grad_ref, lse_ref, div_ref,
+    h_buf, w_buf, kept, kept_x, send_q, recv_q, send_x, recv_x, grads, send_d, top_buf, total,
     stat_send, stat_recv, fin_send, fin_recv,
-    core_send, core_recv, x_send, x_recv, t_buf, up_send, up_recv, down_send, down_recv,
+    core_send, core_recv, x_send, x_recv, t_buf, z_send, z_recv,
     w_sem, gz_up, gz_down, gz_recv, gx_send, gx_recv, gc_send, gc_recv,
-    q_send_sem, q_recv_sem, d_send_sem, d_recv_sem, s_send_sem, s_recv_sem, f_sem,
-    rc_send, rc_recv, rx_send, rx_recv, ru_send, ru_recv, rd_send, rd_recv,
+    q_send_sem, q_recv_sem, e_send_sem, e_recv_sem, d_send_sem, d_recv_sem, s_send_sem, s_recv_sem, f_sem,
+    rc_send, rc_recv, rx_send, rx_recv, rz_send, rz_recv,
 ):
     wide = lax.axis_index("wide")
     z = lax.axis_index("narrow")
@@ -202,125 +205,145 @@
     def peer(i):
         return at(base + i // line, i % line)
 
+    passing = chunks - HELD
+
+    def fetch(chunk, slot):
+        col = pl.multiple_of(chunk * WIDTH, WIDTH)
+        return pltpu.make_async_copy(w_ref.at[:, pl.ds(col, WIDTH)], w_buf.at[slot], w_sem.at[slot])
+
+    def held(chunk):
+        return fetch(chunk, RING + chunk)
+
     def weights(t):
-        col = pl.multiple_of(t % chunks * WIDTH, WIDTH)
-        slot = t % SLOTS
-        return pltpu.make_async_copy(w_ref.at[:, pl.ds(col, WIDTH)], w_buf.at[slot], w_sem.at[slot])
-
-    for t in range(SLOTS - 1):
+        return fetch(HELD + t % passing, t % RING)
+
+    @pl.loop(0, HELD)
+    def _(c):
+        held(c).start()
+
+    for t in range(RING - 1):
         weights(t).start()
 
     barrier = pltpu.get_barrier_semaphore()
-    pl.semaphore_signal(barrier, inc=1, device_id=across, device_id_type=MESH)
-
-    @pl.loop(1, members)
-    def _(i):
-        pl.semaphore_signal(
-            barrier, inc=1, device_id=peer((me + i) % members), device_id_type=MESH
-        )
-
-    pl.semaphore_wait(barrier, members)
-
-    def place(cx, cc, cz):
+    for to in (core_side, x_side, across):
+        pl.semaphore_signal(barrier, inc=1, device_id=to, device_id_type=MESH)
+
+    @pl.when(z > 0)
+    def _():
+        pl.semaphore_signal(barrier, inc=1, device_id=below, device_id_type=MESH)
+
+    @pl.when(z < line - 1)
+    def _():
+        pl.semaphore_signal(barrier, inc=1, device_id=above, device_id_type=MESH)
+
+    at_end = jnp.logical_or(z == 0, z == line - 1)
+
+    @pl.when(at_end)
+    def _():
+        pl.semaphore_wait(barrier, 4)
+
+    @pl.when(jnp.logical_not(at_end))
+    def _():
+        pl.semaphore_wait(barrier, 5)
+
+    piece = rows // PIECES
+
+    def place(cx, cc, cz, p):
         pos = (cc + head - 2 * cc * head) * sides + cx
         return h_buf.at[
-            pl.ds(pl.multiple_of(pos * rows, rows), rows),
+            pl.ds(pl.multiple_of(pos * rows + p * piece, piece), piece),
             pl.ds(pl.multiple_of(cz * feats, feats), feats),
         ]
 
-    def push(cx, cc, cz, own, send, recv, to):
-        src = hid_ref if own else place(cx, cc, cz)
+    def push(cx, cc, cz, p, own, send, recv, to):
+        src = hid_ref.at[pl.ds(p * piece, piece)] if own else place(cx, cc, cz, p)
         return pltpu.make_async_remote_copy(
-            src_ref=src, dst_ref=place(cx, cc, cz), send_sem=send, recv_sem=recv,
+            src_ref=src, dst_ref=place(cx, cc, cz, p), send_sem=send, recv_sem=recv,
             device_id=to, device_id_type=MESH,
         )
 
-    def g_up(cz, own=False):
-        return push(x, core, cz, own, gz_up.at[cz], gz_recv.at[cz], above)
-
-    def g_down(cz, own=False):
-        return push(x, core, cz, own, gz_down.at[cz], gz_recv.at[cz], below)
-
-    def g_x(cz, own=False):
-        return push(x, core, cz, own, gx_send.at[cz], gx_recv.at[cz], x_side)
-
-    def g_x_in(cz):
-        return push(1 - x, core, cz, False, gx_send.at[cz], gx_recv.at[cz], x_side)
-
-    def g_c(cx, cz, own=False):
-        return push(cx, core, cz, own, gc_send.at[cx, cz], gc_recv.at[cx, cz], core_side)
-
-    def g_c_in(cx, cz):
-        return push(cx, 1 - core, cz, False, gc_send.at[cx, cz], gc_recv.at[cx, cz], core_side)
-
-    @pl.when(z < line - 1)
-    def _():
-        g_up(z, True).start()
-
-    @pl.when(z > 0)
-    def _():
-        g_down(z, True).start()
-
-    g_x(z, True).start()
-    g_c(x, z, True).start()
-    place(x, core, z)[...] = hid_ref[...]
-
-    def from_x(cz):
-        g_x_in(cz).wait_recv()
-        g_c(1 - x, cz).start()
-
-    for s in range(1, line):
-        @pl.when(z - s >= 0)
-        def _():
-            g_up(z - s).wait_recv()
-
-            @pl.when(z < line - 1)
-            def _():
-                g_up(z - s).start()
-
-            g_x(z - s).start()
-            g_c(x, z - s).start()
-
-        @pl.when(z + s < line)
-        def _():
-            g_down(z + s).wait_recv()
-
-            @pl.when(z > 0)
-            def _():
-                g_down(z + s).start()
-
-            g_x(z + s).start()
-            g_c(x, z + s).start()
-
-        if s == 1:
-            from_x(z)
-        else:
-            @pl.when(z - s + 1 >= 0)
-            def _():
-                from_x(z - s + 1)
-
-            @pl.when(z + s - 1 < line)
-            def _():
-                from_x(z + s - 1)
-
-    last = line - 1
-
-    if last > 0:
-        @pl.when(z - last >= 0)
-        def _():
-            from_x(z - last)
-
-        @pl.when(z + last < line)
-        def _():
-            from_x(z + last)
-    else:
-        from_x(z)
+    def g_up(cz, p, own=False):
+        return push(x, core, cz, p, own, gz_up.at[cz, p], gz_recv.at[cz, p], above)
+
+    def g_down(cz, p, own=False):
+        return push(x, core, cz, p, own, gz_down.at[cz, p], gz_recv.at[cz, p], below)
+
+    def g_x(cz, p, own=False):
+        return push(x, core, cz, p, own, gx_send.at[cz, p], gx_recv.at[cz, p], x_side)
+
+    def g_x_in(cz, p):
+        return push(1 - x, core, cz, p, False, gx_send.at[cz, p], gx_recv.at[cz, p], x_side)
+
+    def g_c(cx, cz, p, own=False):
+        return push(cx, core, cz, p, own, gc_send.at[cx, cz, p], gc_recv.at[cx, cz, p], core_side)
+
+    def g_c_in(cx, cz, p):
+        return push(
+            cx, 1 - core, cz, p, False, gc_send.at[cx, cz, p], gc_recv.at[cx, cz, p], core_side
+        )
+
+    mine = core + head - 2 * core * head
+
+    for p in range(PIECES):
+        @pl.when(z < line - 1)
+        def _():
+            g_up(z, p, True).start()
+
+        @pl.when(z > 0)
+        def _():
+            g_down(z, p, True).start()
+
+        g_x(z, p, True).start()
+        g_c(x, z, p, True).start()
+        place(x, core, z, p)[...] = hid_ref[p * piece : (p + 1) * piece]
 
     total[...] = jnp.zeros_like(total)
     top_buf[...] = jnp.full_like(top_buf, -1e30)
+
+    def from_x(cz, p):
+        g_x_in(cz, p).wait_recv()
+        g_c(1 - x, cz, p).start()
+
+    for s in range(1, line + 1):
+        for p in range(PIECES):
+            if s < line:
+                @pl.when(z - s >= 0)
+                def _():
+                    g_up(z - s, p).wait_recv()
+
+                    @pl.when(z < line - 1)
+                    def _():
+                        g_up(z - s, p).start()
+
+                    g_x(z - s, p).start()
+                    g_c(x, z - s, p).start()
+
+                @pl.when(z + s < line)
+                def _():
+                    g_down(z + s, p).wait_recv()
+
+                    @pl.when(z > 0)
+                    def _():
+                        g_down(z + s, p).start()
+
+                    g_x(z + s, p).start()
+                    g_c(x, z + s, p).start()
+
+            if s == 1:
+                from_x(z, p)
+            else:
+                @pl.when(z - s + 1 >= 0)
+                def _():
+                    from_x(z - s + 1, p)
+
+                @pl.when(z + s - 1 < line)
+                def _():
+                    from_x(z + s - 1, p)
+
     for cz in range(line):
         for cx in range(sides):
-            g_c_in(cx, cz).wait_recv()
+            for p in range(PIECES):
+                g_c_in(cx, cz, p).wait_recv()
 
     reach = 2.0 * depth * HIDDEN_MAX * WEIGHT_MAX + 2.0
     code_scale = float(int(65500.0 / reach ** 0.25))
@@ -331,22 +354,44 @@
             recv_sem=q_recv_sem.at[j], device_id=across, device_id_type=MESH,
         )
 
+    def extra_copy(i):
+        return pltpu.make_async_remote_copy(
+            src_ref=send_x.at[i], dst_ref=recv_x.at[i], send_sem=e_send_sem.at[i],
+            recv_sem=e_recv_sem.at[i], device_id=across, device_id_type=MESH,
+        )
+
+    def encode(ref, j, values, top):
+        top_code = jnp.floor(top * 0.5) + 1.0
+        gap = jnp.sqrt(jnp.sqrt(jnp.maximum(2.0 * top_code - values, 0.0)))
+        code = (gap * code_scale + 0.5).astype(jnp.int32) - 32768
+        ref[j, 0:WIDTH] = code.astype(jnp.int16)
+        ref[j, WIDTH:] = jnp.broadcast_to(top_code.astype(jnp.int32), (16, half)).astype(jnp.int16)
+
+    def slot_of(j):
+        return jnp.where(j < HELD, RING + j, (j - HELD) % RING)
+
     @pl.loop(0, chunks)
     def _(j):
-        weights(j + SLOTS - 1).start()
-        weights(j).wait()
-        logits = jnp.dot(h_buf[...], w_buf[j % SLOTS], preferred_element_type=F32)
-        kept[j] = logits[:half].T
-        other = logits[half:].T
+        @pl.when(j < HELD)
+        def _():
+            held(j).wait()
+
+        @pl.when(j >= HELD)
+        def _():
+            weights(j - HELD + RING - 1).start()
+            weights(j - HELD).wait()
+
+        logits = jnp.dot(h_buf[...], w_buf[slot_of(j)], preferred_element_type=F32)
+        own, other = logits[:half].T, logits[half:].T
+        kept[j] = own
         top = jnp.maximum(top_buf[...], jnp.max(other, 0, keepdims=True))
         top_buf[...] = top
-        top_code = jnp.floor(top * 0.5) + 1.0
-        gap = jnp.sqrt(jnp.sqrt(jnp.maximum(2.0 * top_code[0:1] - other, 0.0)))
-        code = (gap * code_scale + 0.5).astype(jnp.int32) - 32768
-        send_q[j, 0:WIDTH] = code.astype(jnp.int16)
-        send_q[j, WIDTH:] = jnp.broadcast_to(
-            top_code[0:1].astype(jnp.int32), (16, half)
-        ).astype(jnp.int16)
+        encode(send_q, j, other, top[0:1])
+
+        @pl.when(jnp.logical_and(j >= HELD, j < HELD + BOTH))
+        def _():
+            kept_x[j - HELD] = other
+            encode(send_x, j - HELD, own, jnp.max(own, 0, keepdims=True))
 
         @pl.when(j > 0)
         def _():
@@ -354,16 +399,22 @@
 
     q_copy(chunks - 1).start()
 
-    def load_pair(j):
-        own = kept[j]
-        code = recv_q[j, 0:WIDTH].astype(jnp.int32).astype(F32) + 32768.0
-        top = recv_q[j, WIDTH:].astype(jnp.int32).astype(F32)[0:1] * 2.0
+    @pl.loop(0, BOTH)
+    def _(i):
+        extra_copy(i).start()
+
+    def pair(ours, ref, j):
+        code = ref[j, 0:WIDTH].astype(jnp.int32).astype(F32) + 32768.0
+        top = ref[j, WIDTH:].astype(jnp.int32).astype(F32)[0:1] * 2.0
         gap = code * (1.0 / code_scale)
         gap = gap * gap
-        other = top - gap * gap
-        policy = jnp.where(is_ref, other, own)
-        ref = jnp.where(is_ref, own, other)
+        theirs = top - gap * gap
+        policy = jnp.where(is_ref, theirs, ours)
+        ref = jnp.where(is_ref, ours, theirs)
         return policy, (1.0 - BETA) * policy + BETA * ref
+
+    def load_pair(j):
+        return pair(kept[j], recv_q, j)
 
     def stat_step(j, carry):
         p_top, m_top, p_sum, m_sum, cross = carry
@@ -423,12 +474,27 @@
     policy_lse = p_top + jnp.log(p_sum)
     mixture_lse = m_top + jnp.log(m_sum)
     divergence = cross / p_sum - policy_lse + mixture_lse
-    finals = jnp.concatenate([mixture_lse, divergence] + [zero] * 6, 0)
+    finals = jnp.concatenate([mixture_lse, divergence, policy_lse] + [zero] * 5, 0)
     fin_send[...] = finals
 
-    kl = kl_ref[pl.ds(head, 1), :]
-    adv = adv_ref[pl.ds(head, 1), :]
-    ids = ids_ref[pl.ds(head, 1), :] - me * width
+    place_lane = lax.broadcasted_iota(jnp.int32, (1, half), 1)
+
+    def own_row(ref, second_half):
+        first, second = ref[0:half].reshape(1, half), ref[half:].reshape(1, half)
+        low_part = jnp.where(place_lane < rows, first, pltpu.roll(second, rows, 1))
+        high_part = jnp.where(place_lane < rows, pltpu.roll(first, rows, 1), second)
+        return jnp.where(second_half, high_part, low_part)
+
+    base_col = me * width
+
+    def row_values(second_half):
+        return (
+            own_row(kl_ref, second_half),
+            own_row(adv_ref, second_half),
+            own_row(ids_ref, second_half) - base_col,
+        )
+
+    ours = row_values(is_ref) + (policy_lse, mixture_lse, divergence)
     col = lax.broadcasted_iota(jnp.int32, (WIDTH, half), 0)
 
     def d_copy(j):
@@ -437,63 +503,101 @@
             recv_sem=d_recv_sem.at[j], device_id=across, device_id_type=MESH,
         )
 
-    def grad_step(j):
-        policy, mixed = load_pair(j)
-        policy_prob = jnp.exp(policy - policy_lse)
-        mixture_prob = jnp.exp(mixed - mixture_lse)
-        log_gap = policy - policy_lse - mixed + mixture_lse
+    def grads_of(j, policy, mixed, values):
+        kl, adv, ids, p_lse, m_lse, div = values
+        policy_prob = jnp.exp(policy - p_lse)
+        mixture_prob = jnp.exp(mixed - m_lse)
+        log_gap = policy - p_lse - mixed + m_lse
         chosen = jnp.where(col + j * WIDTH == ids, 1.0, 0.0)
         shift = mixture_prob - policy_prob
         policy_grad = kl * (
-            policy_prob * (log_gap - divergence) + (1.0 - BETA) * shift
+            policy_prob * (log_gap - div) + (1.0 - BETA) * shift
         ) - adv * (chosen - policy_prob)
-        ref_grad = BETA * kl * shift
+        return policy_grad, BETA * kl * shift
+
+    def grad_step(j):
+        policy, mixed = load_pair(j)
+        policy_grad, ref_grad = grads_of(j, policy, mixed, ours)
         grads[j, 0] = jnp.where(is_ref, ref_grad, policy_grad).astype(BF16)
         send_d[j] = jnp.where(is_ref, policy_grad, ref_grad).astype(BF16)
 
-        @pl.when(j > 0)
-        def _():
-            d_copy(j - 1).start()
-
-        @pl.when(j == chunks - 1)
-        def _():
-            d_copy(j).start()
-
-    @pl.loop(0, min(AHEAD, chunks))
-    def _(j):
-        grad_step(j)
+    first_sent = HELD + BOTH
+    sent = passing - BOTH
+
+    def send_grad(k):
+        @pl.when(k < sent)
+        def _():
+            d_copy(first_sent + k).start()
+
+        @pl.when(jnp.logical_and(k >= sent, k < sent + HELD))
+        def _():
+            d_copy(k - sent).start()
 
     f_copy = pltpu.make_async_remote_copy(
         src_ref=fin_send, dst_ref=fin_recv, send_sem=f_sem.at[0], recv_sem=f_sem.at[1],
         device_id=across, device_id_type=MESH,
     )
-    f_copy.start()
-
-    block = depth // 8
-
-    @pl.loop(0, chunks)
-    def _(j):
-        @pl.when(j + AHEAD < chunks)
-        def _():
-            grad_step(j + AHEAD)
-
-        @pl.when(j + SLOTS - 1 < chunks)
-        def _():
-            weights(chunks + j + SLOTS - 1).start()
-
-        weights(chunks + j).wait()
-        d_copy(j).wait_recv()
+
+    @pl.loop(0, AHEAD)
+    def _(k):
+        grad_step(first_sent + k)
+
+        @pl.when(k > 0)
+        def _():
+            d_copy(first_sent + k - 1).start()
+
+        @pl.when(k == 0)
+        def _():
+            f_copy.start()
+
+    def add(part, slot, rhs):
+        total[part] += jnp.dot(w_buf[slot], rhs, preferred_element_type=F32)
+
+    f_copy.wait_recv()
+    row_stats = fin_recv[...]
+    theirs = row_values(jnp.logical_not(is_ref)) + (
+        row_stats[2:3], row_stats[0:1], row_stats[1:2]
+    )
+
+    @pl.loop(0, passing)
+    def _(t):
+        j = HELD + t
+        k = t + AHEAD
+
+        @pl.when(k < sent)
+        def _():
+            grad_step(first_sent + k)
+
+        send_grad(k - 1)
+
+        @pl.when(t + RING - 1 < passing)
+        def _():
+            weights(passing + t + RING - 1).start()
+
+        weights(passing + t).wait()
+
+        @pl.when(t < BOTH)
+        def _():
+            grad_step(j)
+            extra_copy(t).wait_recv()
+            policy, mixed = pair(kept_x[t], recv_x, t)
+            policy_grad, ref_grad = grads_of(j, policy, mixed, theirs)
+            grads[j, 1] = jnp.where(is_ref, ref_grad, policy_grad).astype(BF16)
+
+        @pl.when(jnp.logical_and(t >= BOTH, t < BOTH + HELD))
+        def _():
+            grad_step(t - BOTH)
+            add(0, RING + t - BOTH, grads[t - BOTH, 0])
+
+        @pl.when(t >= BOTH)
+        def _():
+            d_copy(j).wait_recv()
+
         rhs = jnp.concatenate([grads[j, 0], grads[j, 1]], 1)
-        slot = (chunks + j) % SLOTS
-
-        @pl.loop(0, 8)
-        def _(b):
-            span = pl.ds(pl.multiple_of(b * block, block), block)
-            term = jnp.dot(w_buf[slot, span], rhs, preferred_element_type=F32)
-            total[0, span] += term[:, :half]
-            total[1, span] += term[:, half:]
-
-    mine = core + head - 2 * core * head
+        term = jnp.dot(w_buf[(passing + t) % RING], rhs, preferred_element_type=F32)
+        total[0] += term[:, :half]
+        total[1] += term[:, half:]
+
     fold = feats // 2
     lane = lax.broadcasted_iota(jnp.int32, (fold, half), 1)
 
@@ -521,20 +625,18 @@
     def r_x(cz):
         return hand(x_send.at[cz], x_recv.at[cz], rx_send.at[cz], rx_recv.at[cz], x_side)
 
-    def r_up(cz):
-        return hand(up_send.at[cz], up_recv.at[cz], ru_send.at[cz], ru_recv.at[cz], above)
-
-    def r_down(cz):
-        return hand(down_send.at[cz], down_recv.at[cz], rd_send.at[cz], rd_recv.at[cz], below)
-
-    @pl.loop(0, line)
-    def _(k):
+    def r_z(cz):
+        return hand(z_send.at[cz], z_recv.at[z], rz_send.at[cz], rz_recv.at[z], at(wide, cz))
+
+    def r_z_in(cz):
+        return hand(z_send.at[cz], z_recv.at[cz], rz_send.at[cz], rz_recv.at[cz], at(wide, cz))
+
+    def to_core(k):
         cz = order(k)
         core_send[cz] = total[1 - mine, span_of(cz)].astype(BF16)
         r_core(cz).start()
 
-    @pl.loop(0, line)
-    def _(k):
+    def to_x(k):
         cz = order(k)
         r_core(cz).wait_recv()
         upper = total[mine, span_of(cz, 0)] + core_recv[cz, 0:fold].astype(F32)
@@ -545,97 +647,109 @@
         x_send[cz] = jnp.where(x == 0, right, left).astype(BF16)
         r_x(cz).start()
 
-    def settled(cz):
+    def to_z(k):
+        cz = order(k)
         r_x(cz).wait_recv()
-        t_buf[cz] += x_recv[cz].astype(F32)
-
-    def go_up(cz):
-        settled(cz)
-
-        @pl.when(z > 0)
-        def _():
-            r_up(cz).wait_recv()
-            t_buf[cz] += up_recv[cz].astype(F32)
-
-        up_send[cz] = t_buf[cz].astype(BF16)
-        r_up(cz).start()
-
-    def go_down(cz):
-        settled(cz)
-
-        @pl.when(z < line - 1)
-        def _():
-            r_down(cz).wait_recv()
-            t_buf[cz] += down_recv[cz].astype(F32)
-
-        down_send[cz] = t_buf[cz].astype(BF16)
-        r_down(cz).start()
-
-    @pl.loop(0, line - 1)
+        z_send[cz] = (t_buf[cz] + x_recv[cz].astype(F32)).astype(BF16)
+        r_z(cz).start()
+
+    @pl.loop(0, HELD)
+    def _(j):
+        send_grad(passing + j + AHEAD - 1)
+
+        @pl.when(jnp.logical_and(mine == 1, j == 0))
+        def _():
+            @pl.loop(0, line)
+            def _(k):
+                to_core(k)
+
+        @pl.when(jnp.logical_and(mine == 0, jnp.logical_and(j >= 2, j < 2 + line)))
+        def _():
+            to_x(j - 2)
+
+        @pl.when(jnp.logical_and(mine == 0, jnp.logical_and(j >= 5, j < 4 + line)))
+        def _():
+            to_z(j - 5)
+
+        d_copy(j).wait_recv()
+        add(1, RING + j, grads[j, 1])
+
+    @pl.when(mine == 0)
+    def _():
+        @pl.loop(0, line)
+        def _(k):
+            to_core(k)
+
+    @pl.when(mine == 1)
+    def _():
+        @pl.loop(0, line)
+        def _(k):
+            to_x(k)
+
+        @pl.loop(0, line - 1)
+        def _(k):
+            to_z(k)
+
+    r_x(z).wait_recv()
+    t_buf[z] += x_recv[z].astype(F32)
+
+    @pl.loop(1, line)
     def _(i):
-        @pl.when(line - 1 - i > z)
-        def _():
-            go_up(line - 1 - i)
-
-        @pl.when(i < z)
-        def _():
-            go_down(i)
-
-    settled(z)
-
-    @pl.when(z > 0)
-    def _():
-        r_up(z).wait_recv()
-        t_buf[z] += up_recv[z].astype(F32)
-
-    @pl.when(z < line - 1)
-    def _():
-        r_down(z).wait_recv()
-        t_buf[z] += down_recv[z].astype(F32)
+        cz = (z + i) % line
+        r_z_in(cz).wait_recv()
+        t_buf[z] += z_recv[cz].astype(F32)
 
     done = t_buf[z]
     grad_ref[0:fold] = done[:, 0:rows]
     grad_ref[fold:] = pltpu.roll(done, rows, 1)[:, 0:rows]
 
-    f_copy.wait_recv()
-    theirs = fin_recv[...]
-    row_ref[0] = jnp.where(is_ref, theirs, finals)
-    row_ref[1] = jnp.where(is_ref, finals, theirs)
+    even, odd = jnp.where(is_ref, row_stats, finals), jnp.where(is_ref, finals, row_stats)
+    wide_lane = lax.broadcasted_iota(jnp.int32, (8, half), 1)
+    first = jnp.where(wide_lane < rows, even, pltpu.roll(odd, rows, 1))
+    second = jnp.where(wide_lane < rows, pltpu.roll(even, rows, 1), odd)
+    lse_ref[0:half] = first[0]
+    lse_ref[half:] = second[0]
+    div_ref[0:half] = first[1]
+    div_ref[half:] = second[1]
 
     f_copy.wait_send()
 
     @pl.loop(0, chunks)
     def _(j):
         q_copy(j).wait_send()
-        d_copy(j).wait_send()
+
+        @pl.when(jnp.logical_or(j < HELD, j >= first_sent))
+        def _():
+            d_copy(j).wait_send()
+
+    @pl.loop(0, BOTH)
+    def _(i):
+        extra_copy(i).wait_send()
 
     @pl.loop(1, members)
     def _(i):
         s_copy((me + i) % members).wait_send()
+
+    @pl.loop(1, line)
+    def _(i):
+        r_z((z + i) % line).wait_send()
 
     @pl.loop(0, line)
     def _(cz):
         r_core(cz).wait_send()
         r_x(cz).wait_send()
-        g_x(cz).wait_send()
-        for cx in range(sides):
-            g_c(cx, cz).wait_send()
-
-        @pl.when(cz > z)
-        def _():
-            r_up(cz).wait_send()
-
-        @pl.when(cz < z)
-        def _():
-            r_down(cz).wait_send()
-
-        @pl.when(jnp.logical_and(cz <= z, z < line - 1))
-        def _():
-            g_up(cz).wait_send()
-
-        @pl.when(jnp.logical_and(cz >= z, z > 0))
-        def _():
-            g_down(cz).wait_send()
+        for p in range(PIECES):
+            g_x(cz, p).wait_send()
+            for cx in range(sides):
+                g_c(cx, cz, p).wait_send()
+
+            @pl.when(jnp.logical_and(cz <= z, z < line - 1))
+            def _():
+                g_up(cz, p).wait_send()
+
+            @pl.when(jnp.logical_and(cz >= z, z > 0))
+            def _():
+                g_down(cz, p).wait_send()
 
 
 def fused(hidden, head_weights, token_ids, kl_weight, advantage):
@@ -645,29 +759,27 @@
     tokens = rows * quarter
     half, sides = tokens // 2, quarter // 2
     chunks, members, fold = width // WIDTH, quarter * line, feats // 2
-
-    def split(values):
-        return values.reshape(sides, 2, rows).transpose(1, 0, 2).reshape(2, half)
-
-    def join(values):
-        return values.reshape(2, sides, rows).transpose(1, 0, 2).reshape(tokens)
-
     vmem = pl.BlockSpec(memory_space=pltpu.VMEM)
     dma, v = pltpu.SemaphoreType.DMA, pltpu.VMEM
-    grad, per_row = pl.pallas_call(
+    along = dma((line, PIECES))
+    return pl.pallas_call(
         functools.partial(step_kernel, quarter, line),
         out_shape=(
             jax.ShapeDtypeStruct((feats, rows), F32),
-            jax.ShapeDtypeStruct((2, 8, half), F32),
+            jax.ShapeDtypeStruct((tokens,), F32),
+            jax.ShapeDtypeStruct((tokens,), F32),
         ),
         in_specs=[vmem, pl.BlockSpec(memory_space=pl.ANY), vmem, vmem, vmem],
-        out_specs=(vmem, vmem),
+        out_specs=(vmem, vmem, vmem),
         scratch_shapes=[
             v((tokens, depth), BF16),
-            v((SLOTS, depth, WIDTH), BF16),
+            v((RING + HELD, depth, WIDTH), BF16),
             v((chunks, WIDTH, half), F32),
+            v((BOTH, WIDTH, half), F32),
             v((chunks, WIDTH + 16, half), jnp.int16),
             v((chunks, WIDTH + 16, half), jnp.int16),
+            v((BOTH, WIDTH + 16, half), jnp.int16),
+            v((BOTH, WIDTH + 16, half), jnp.int16),
             v((chunks, 2, WIDTH, half), BF16),
             v((chunks, WIDTH, half), BF16),
             v((8, half), F32),
@@ -683,22 +795,18 @@
             v((line, fold, half), F32),
             v((line, fold, half), BF16),
             v((line, fold, half), BF16),
-            v((line, fold, half), BF16),
-            v((line, fold, half), BF16),
-            dma((SLOTS,)),
-            dma((line,)), dma((line,)), dma((line,)), dma((line,)), dma((line,)),
-            dma((sides, line)), dma((sides, line)),
-            dma((chunks,)), dma((chunks,)), dma((chunks,)), dma((chunks,)),
+            dma((RING + HELD,)),
+            along, along, along, along, along,
+            dma((sides, line, PIECES)), dma((sides, line, PIECES)),
+            dma((chunks,)), dma((chunks,)), dma((BOTH,)), dma((BOTH,)), dma((chunks,)), dma((chunks,)),
             dma((members,)), dma((members,)), dma((2,)),
-            dma((line,)), dma((line,)), dma((line,)), dma((line,)),
-            dma((line,)), dma((line,)), dma((line,)), dma((line,)),
+            dma((line,)), dma((line,)), dma((line,)), dma((line,)), dma((line,)), dma((line,)),
         ],
         compiler_params=pltpu.CompilerParams(
             collective_id=0, has_side_effects=True, vmem_limit_bytes=62 * 1024 * 1024
         ),
         name="step",
-    )(hidden, head_weights, split(token_ids), split(kl_weight), split(advantage))
-    return grad, join(per_row[:, 0]), join(per_row[:, 1])
+    )(hidden, head_weights, token_ids, kl_weight, advantage)
 
 
 def fits(quarter, line, hidden, head_weights):
@@ -709,7 +817,10 @@
         and line >= 2
         and rows * quarter == 2 * LANES
         and width % WIDTH == 0
-        and width // WIDTH >= SLOTS
+        and rows % (16 * PIECES) == 0
+        and width // WIDTH >= 2 * HELD + 2 * BOTH
+        and AHEAD < HELD
+        and line + 4 <= HELD
         and depth % (8 * LANES) == 0
         and feats % 32 == 0
         and feats * line == depth

time: 204 us -> 153 us (0.75); the launches traced: 201 us -> 152 us
  Pallas kernels: 192 us -> 147 us
  local copies, waits for them, and re-layouts: 8.41 us -> 4.36 us
    pallas_call x1, Pallas kernels: 192 us -> 147 us  [fused(): pl.pallas_call(functools.partial(step_kernel, quarter, line), out_shape=(...]
    reshape x8 -> x0, local copies, waits for them, and re-layouts: 5.5 us -> none  [the longest x6 4.21 us: split(): return values.reshape(sides, 2, rows).transpose(1, 0, 2).reshape(2, half)]
where the time goes in v2:
time: 153 us; the launch traced here: 152 us
  Pallas kernels  147 us (96%)
  local copies, waits for them, and re-layouts  4.36 us (3%)
    pallas_call x1, Pallas kernels, fused(): pl.pallas_call(functools.partial(step_kernel, quarter, line), out_shape=(...  147 us

profile of v2, /device:TPU:1, one launch (start us, length us, event | category | flops | bytes accessed | tf_op | source)
XLA Modules:
  0.0 152.5 jit_solution(1420637709638313385)
XLA Ops:
  0.6 147.5 %step.1 = (f32[1024,64]{1,0:T(8,128)}, f32[256]{0:T(256)}, f32[256]{0:T(256)}) custom-call(bf16[64,1024]{1,0:T(8,128)(2,1)} %hid_ref.1, bf16[4096,9472]{1,0:T(8,128)(2,1)} %w_ref.1, s32[256]{0:T(256)} %ids_ref.1, f32[256]{0:T(256)} %kl_ref.1, f32[256]{0:T(256)} %adv_ref.1), custom_call_target="tpu_custom_call" | custom-call | tf_op jit(solution)/shard_map/step/pallas_call | solution.py:765
  148.1 1.9 %copy.8 = f32[1024,64]{0,1:T(8,128)} copy(f32[1024,64]{1,0:T(8,128)} %get-tuple-element.3) | data formatting | bytes 524288 | tf_op jit(solution)/shard_map/step/pallas_call | solution.py:765
  150.0 1.2 copy.11
  151.2 1.2 copy.12
